TPU v7x, 32 devices: a whole 2x2x4 slice. The times are simulated.
32 devices in a mesh: strip: 8 (over z, y), chan: 4 (over x, core).
Axes of the slice: x: 2, y: 2, z: 4, core: 2. Of those that a mesh axis runs over, the one named last changes fastest.
Arguments:
- activations: bfloat16 [64, 128, 1280], P('strip', None, 'chan'), may hold values from -17 to 17
- weight: bfloat16 [9, 1280, 1280], P(None, None, 'chan'), may hold values from -0.0546875 to 0.0546875
- gamma: float32 [1280], replicated, may hold values from 0.25 to 1.75
- beta: float32 [1280], replicated, may hold values from -3 to 3
- group_map: int32 [1280], replicated, may hold values from 0 to 31, as said below
- lengths: int32 [8], P('strip'), may hold values from 1 to 8, 48 in all
- stale_edges: bfloat16 [16, 128, 1280], P('strip', None, 'chan'), may hold values from -6 to 6
- stale_mean: float32 [32], replicated, may hold values from -0.5 to 0.5
- stale_square: float32 [32], replicated, may hold values from 1 to 4
- old_mean: float32 [8, 32], P('strip'), may hold values from -0.5 to 0.5
- old_square: float32 [8, 32], P('strip'), may hold values from 0.5 to 6
Outputs:
- upsampled: bfloat16 [128, 256, 1280], P('strip', None, 'chan')
- new_mean: float32 [32], replicated
- new_square: float32 [32], replicated
Inputs may be any that keep to these rules, and one draw needn't show every extreme that they name: `group_map`: every group has exactly 40 channels. The lengths sum to 48, and some strip uses all 8 rows.
All inputs are finite; a program needn't handle non-finite values. No bound on the sum of `lengths` on one device may be relied on, other than what follows from the above.
Results may differ from a plain program's by a relative error of at most 0.0027.
Values may be sent and summed in bfloat16 or wider, within the bound.
No kernel may reach another device: no remote copies, remote signals or barrier semaphores. Data moves between devices by JAX's collectives and lax.ppermute only.
A program may use at most 64 MiB of HBM per device.

v0:
```python
import jax
import jax.numpy as jnp
from jax import lax
from jax.sharding import PartitionSpec as P

EPS = 1e-05


def padded_2(block, sides, width):
    for axis, dim in sides:
        count = lax.axis_size(axis)
        forward = [(i, i + 1) for i in range(count - 1)]
        backward = [(target, source) for source, target in forward]
        low = lax.ppermute(
            lax.slice_in_dim(block, block.shape[dim] - width, None, axis=dim), axis, forward
        )
        high = lax.ppermute(lax.slice_in_dim(block, 0, width, axis=dim), axis, backward)
        block = jnp.concatenate([low, block, high], axis=dim)
    return block


def per_device(
    activations,
    weight,
    gamma,
    beta,
    group_map,
    lengths,
    stale_edges,
    stale_mean,
    stale_square,
    old_mean,
    old_square,
):
    rows, width, local_c = activations.shape
    channels = weight.shape[1]
    groups = stale_mean.shape[0]
    per_group = channels // groups
    offset = lax.axis_index("chan") * local_c
    member = (group_map[:, None] == jnp.arange(groups, dtype=jnp.int32)[None, :]).astype(
        jnp.float32
    )
    local_member = lax.dynamic_slice_in_dim(member, offset, local_c, 0)
    length = lengths[0]
    used = (jnp.arange(rows, dtype=jnp.int32) < length).astype(jnp.float32)[:, None, None]
    values = activations.astype(jnp.float32) * used
    chan_sum = jnp.sum(values, axis=(0, 1))
    chan_sq = jnp.sum(values * values, axis=(0, 1))
    part_one = jnp.sum(chan_sum[:, None] * local_member, axis=0)
    part_two = jnp.sum(chan_sq[:, None] * local_member, axis=0)
    strip_one, strip_two = lax.psum((part_one, part_two), "chan")
    total_count = float(lax.axis_size("strip") * (3 * rows // 4) * width * per_group)
    image_one, image_two = lax.psum((strip_one, strip_two), "strip")
    new_mean = image_one / total_count
    new_square = image_two / total_count
    count = length.astype(jnp.float32) * (width * per_group)
    fresh_mean = strip_one / count
    fresh_square = strip_two / count
    mean_g = stale_mean + fresh_mean - old_mean[0]
    square_g = stale_square + fresh_square - old_square[0]
    var_g = jnp.maximum(square_g - mean_g * mean_g, 0.5 * (fresh_square - fresh_mean * fresh_mean))
    rstd_g = lax.rsqrt(var_g + EPS)
    scale_c = jnp.sum(member * rstd_g[None, :], axis=1) * gamma
    shift_c = beta - jnp.sum(member * mean_g[None, :], axis=1) * scale_c
    bordered = padded_2(stale_edges, (("strip", 0),), 1)
    bounds = jnp.stack([bordered[0], bordered[3]], axis=0)
    initial = jnp.zeros((rows * width, local_c), jnp.float32)
    total = initial
    piece = lax.all_gather(activations, "chan", axis=2, tiled=True)
    bound = lax.all_gather(bounds, "chan", axis=2, tiled=True)
    depth = piece.shape[2]
    act = (jax.nn.silu(piece.astype(jnp.float32) * scale_c + shift_c) * used).astype(jnp.bfloat16)
    padded = jnp.concatenate([bound[0:1], act, jnp.zeros((1, width, depth), jnp.bfloat16)], axis=0)
    place = (jnp.arange(rows + 2, dtype=jnp.int32) == length + 1)[:, None, None]
    padded = jnp.where(place, bound[1][None], padded)
    padded = jnp.pad(padded, ((0, 0), (1, 1), (0, 0)))
    for tap in range(9):
        down, across = (tap // 3, tap % 3)
        patch = padded[down : down + rows, across : across + width].reshape(rows * width, depth)
        total = total + jnp.dot(patch, weight[tap], preferred_element_type=jnp.float32)
    block = ((activations.astype(jnp.float32) + total.reshape(rows, width, local_c)) * used).astype(
        jnp.bfloat16
    )
    upsampled = jnp.repeat(jnp.repeat(block, 2, axis=0), 2, axis=1)
    return (upsampled, new_mean, new_square)


def solution(mesh):
    in_specs = (
        P("strip", None, "chan"),
        P(None, None, "chan"),
        P(),
        P(),
        P(),
        P("strip"),
        P("strip", None, "chan"),
        P(),
        P(),
        P("strip", None),
        P("strip", None),
    )
    out_specs = (P("strip", None, "chan"), P(), P())
    return jax.shard_map(
        per_device, mesh=mesh, in_specs=in_specs, out_specs=out_specs, check_vma=False
    )
```

profile of v0, /device:TPU:0, one launch (start us, length us, event | category | flops | bytes accessed | tf_op | source)
XLA Modules:
  0.0 100.3 jit_solution(1135148588902950023)
XLA Ops:
  7.2 0.0 copy-start
  7.2 0.0 copy-start.3
  7.2 0.0 copy-start.6
  7.2 0.0 copy-start.8
  7.2 0.0 copy-start.7
  7.2 0.0 copy-start.9
  7.2 0.0 copy-start.4
  7.2 0.0 copy-start.5
  7.2 0.0 all-gather.2.cloned.1.call-start
  7.3 2.4 %copy.49 = bf16[8,128,320]{1,0,2:T(8,128)(2,1)} copy(bf16[8,128,320]{1,2,0:T(8,128)(2,1)} %param.11) | data formatting | bytes 1310720 | tf_op args[0]
  9.7 0.0 all-gather.2.cloned.1.call-update
  9.7 0.9 fusion.30
  10.7 0.1 copy.55
  10.8 1.3 %collective-permute-start.1 = (bf16[1,128,320]{1,0,2:T(2,128)(2,1)S(1)}, bf16[1,128,320]{1,0,2:T(2,128)(2,1)S(1)}, u32[]{:S(2)}, u32[]{:S(2)}) collective-permute-start(bf16[1,128,320]{1,0,2:T(2,128)(2,1)S(1)} %copy.55), channel_id=1, source_target_pairs={{4,0},{8,4},{12,8},{16,12},{20,16},{24,20},{28,24},{5,1},{9,5},{13... | collective-permute-start | bytes 245768 | tf_op jit(solution)/shard_map/ppermute | solution.py:17
  12.1 0.1 copy.54
  12.2 5.5 %collective-permute-start = (bf16[1,128,320]{1,0,2:T(2,128)(2,1)S(1)}, bf16[1,128,320]{1,0,2:T(2,128)(2,1)S(1)}, u32[]{:S(2)}, u32[]{:S(2)}) collective-permute-start(bf16[1,128,320]{1,0,2:T(2,128)(2,1)S(1)} %copy.54), channel_id=1, source_target_pairs={{0,4},{4,8},{8,12},{12,16},{16,20},{20,24},{24,28},{1,5},{5,9},{9,... | collective-permute-start | bytes 245768 | tf_op jit(solution)/shard_map/ppermute | solution.py:14
  18.4 0.1 pad.7.clone
  18.5 0.0 copy-done
  18.5 0.4 fusion.3
  18.9 0.0 copy-done.3
  18.9 0.2 fusion.26
  19.1 7.3 %all-reduce.2 = (f32[32]{0:T(128)S(1)}, f32[32]{0:T(128)S(1)}) all-reduce(f32[32]{0:T(128)S(1)} %get-tuple-element.21, f32[32]{0:T(128)S(1)} %get-tuple-element.20), channel_id=1, replica_groups=mesh['strip'=8,'chan'=4] {'chan'}, use_global_device_ids=true, to_apply=%region_5.0 | all-reduce | flops 64 | bytes 512 | tf_op jit(solution)/shard_map/psum | solution.py:51
  26.5 19.8 %all-reduce.1 = (f32[32]{0:T(128)S(1)}, f32[32]{0:T(128)S(1)}) all-reduce(f32[32]{0:T(128)S(1)} %get-tuple-element.26, f32[32]{0:T(128)S(1)} %get-tuple-element.27), channel_id=1, replica_groups=mesh['strip'=8,'chan'=4] {'strip'}, use_global_device_ids=true, to_apply=%region_8.0 | all-reduce | flops 64 | bytes 512 | tf_op jit(solution)/shard_map/psum | solution.py:53
  46.2 0.0 copy-done.6
  46.2 0.0 copy-done.8
  46.2 0.0 copy-done.7
  46.2 0.0 copy-done.9
  46.3 0.1 select_reduce_fusion.1
  46.4 0.5 broadcast_multiply_fusion
  46.9 0.0 copy-done.4
  46.9 0.0 copy-done.5
  46.9 0.0 collective-permute-done.1
  47.0 0.0 collective-permute-done
  47.0 0.4 pad_maximum_fusion
  47.3 7.5 %all_gather.6 = bf16[2,128,1280]{1,0,2:T(2,128)(2,1)S(1)} all-gather(bf16[2,128,320]{1,0,2:T(2,128)(2,1)S(1)} %pad_maximum_fusion), channel_id=1, replica_groups=mesh['strip'=8,'chan'=4] {'chan'}, dimensions={2}, use_global_device_ids=true | all-gather | bytes 819200 | tf_op jit(solution)/shard_map/all_gather | solution.py:70
  54.9 0.9 fusion.29
  55.8 1.1 %copy.56 = bf16[1,128,1280]{2,1,0:T(8,128)(2,1)} copy(bf16[1,128,1280]{1,0,2:T(2,128)(2,1)S(1)} %get-tuple-element.41) | data formatting | bytes 655360
  56.9 1.1 %copy.57 = bf16[1,128,1280]{2,1,0:T(8,128)(2,1)} copy(bf16[1,128,1280]{1,0,2:T(2,128)(2,1)S(1)} %get-tuple-element.42) | data formatting | bytes 655360
  58.0 3.8 %copy.50 = bf16[8,128,1280]{2,1,0:T(8,128)(2,1)S(1)} copy(bf16[8,128,1280]{1,0,2:T(8,128)(2,1)} %all-gather.2.cloned.1.call-done) | data formatting | bytes 5242880 | tf_op jit(solution)/shard_map/all_gather | solution.py:69
  61.8 0.0 copy-start.1
  61.9 0.0 copy-start.2
  61.9 1.7 %multiply_convert_fusion = bf16[8,128,1280]{2,1,0:T(8,128)(2,1)S(1)} fusion(bf16[8,128,1280]{2,1,0:T(8,128)(2,1)S(1)} %copy.50, f32[8]{0:T(128)S(1)} %compare_convert_fusion, f32[1280]{0:T(1024)S(1)} %get-tuple-element.28, f32[1280]{0:T(1024)S(1)} %get-tuple-element.29), kind=kLoop, calls=%fused_computation | loop fusion | flops 11796480 | bytes 5253152 | tf_op jit(solution)/shard_map/convert_element_type | solution.py:72
  63.5 0.0 copy-done.1
  63.5 0.0 copy-done.2
  63.5 0.4 maximum_select_fusion
  64.0 10.0 %pad_slice_fusion = (bf16[8,128,1280]{2,1,0:T(8,128)(2,1)S(1)}, bf16[8,128,1280]{2,1,0:T(8,128)(2,1)S(1)}, bf16[8,128,1280]{2,1,0:T(8,128)(2,1)S(1)}, bf16[8,128...) fusion(bf16[10,128,1280]{2,1,0:T(8,128)(2,1)S(1)} %maximum_sele, ...), kind=kLoop, calls=%fused_computation.2 | loop fusion | bytes 34734080 | tf_op jit(solution)/shard_map/slice | solution.py:79
  74.1 0.0 slice-start
  74.1 2.3 %fusion.14 = f32[1024,320]{0,1:T(8,128)S(1)} fusion(bf16[1024,1280]{1,0:T(8,128)(2,1)S(1)} %bitcast.78, bf16[9,1280,320]{1,2,0:T(8,128)(2,1)} %param.12), kind=kOutput, calls=%fused_computation.32 | convolution fusion | flops 838860800 | bytes 4751360 | tf_op jit(solution)/shard_map/dot_general | solution.py:80
  76.4 0.0 slice-start.1
  76.4 2.3 %convolution_add_fusion.7 = f32[1024,320]{0,1:T(8,128)S(1)} fusion(f32[1024,320]{0,1:T(8,128)S(1)} %fusion.14, bf16[1024,1280]{1,0:T(8,128)(2,1)S(1)} %bitcast.77, bf16[9,1280,320]{1,2,0:T(8,128)(2,1)} %param.12), kind=kOutput, calls=%fused_computation.20 | convolution fusion | flops 839188480 | bytes 6062080 | tf_op jit(solution)/shard_map/dot_general | solution.py:80
  78.8 0.0 slice-done
  78.8 0.0 slice-done.1
  78.8 1.1 %convolution_add_fusion.6 = f32[1024,320]{0,1:T(8,128)S(1)} fusion(f32[1024,320]{0,1:T(8,128)S(1)} %convolution_add_fusion.7, bf16[1024,1280]{1,0:T(8,128)(2,1)S(1)} %bitcast.76, bf16[9,1280,320]{1,2,0:T(8,128)(2,1)S(1)} %bitcast.81), kind=kOutput, calls=%fused_computation.19 | convolution fusion | flops 839188480 | bytes 6062080 | tf_op jit(solution)/shard_map/dot_general | solution.py:80
  79.9 1.0 %convolution_add_fusion.5 = f32[1024,320]{0,1:T(8,128)S(1)} fusion(f32[1024,320]{0,1:T(8,128)S(1)} %convolution_add_fusion.6, bf16[1024,1280]{1,0:T(8,128)(2,1)S(1)} %bitcast.75, bf16[9,1280,320]{1,2,0:T(8,128)(2,1)S(1)} %bitcast.81), kind=kOutput, calls=%fused_computation.18 | convolution fusion | flops 839188480 | bytes 6062080 | tf_op jit(solution)/shard_map/dot_general | solution.py:80
  80.9 1.1 %convolution_add_fusion.4 = f32[1024,320]{0,1:T(8,128)S(1)} fusion(f32[1024,320]{0,1:T(8,128)S(1)} %convolution_add_fusion.5, bf16[1024,1280]{1,0:T(8,128)(2,1)S(1)} %bitcast.74, bf16[9,1280,320]{1,2,0:T(8,128)(2,1)S(1)} %bitcast.81), kind=kOutput, calls=%fused_computation.17 | convolution fusion | flops 839188480 | bytes 6062080 | tf_op jit(solution)/shard_map/dot_general | solution.py:80
  82.0 1.1 %convolution_add_fusion.3 = f32[1024,320]{0,1:T(8,128)S(1)} fusion(f32[1024,320]{0,1:T(8,128)S(1)} %convolution_add_fusion.4, bf16[1024,1280]{1,0:T(8,128)(2,1)S(1)} %bitcast.73, bf16[9,1280,320]{1,2,0:T(8,128)(2,1)S(1)} %bitcast.81), kind=kOutput, calls=%fused_computation.16 | convolution fusion | flops 839188480 | bytes 6062080 | tf_op jit(solution)/shard_map/dot_general | solution.py:80
  83.0 1.1 %convolution_add_fusion.2 = f32[1024,320]{0,1:T(8,128)S(1)} fusion(f32[1024,320]{0,1:T(8,128)S(1)} %convolution_add_fusion.3, bf16[1024,1280]{1,0:T(8,128)(2,1)S(1)} %bitcast.72, bf16[9,1280,320]{1,2,0:T(8,128)(2,1)S(1)} %bitcast.81), kind=kOutput, calls=%fused_computation.15 | convolution fusion | flops 839188480 | bytes 6062080 | tf_op jit(solution)/shard_map/dot_general | solution.py:80
  84.1 1.1 %convolution_add_fusion.1 = f32[1024,320]{0,1:T(8,128)S(1)} fusion(f32[1024,320]{0,1:T(8,128)S(1)} %convolution_add_fusion.2, bf16[1024,1280]{1,0:T(8,128)(2,1)S(1)} %bitcast.71, bf16[9,1280,320]{1,2,0:T(8,128)(2,1)S(1)} %bitcast.81), kind=kOutput, calls=%fused_computation.14 | convolution fusion | flops 839188480 | bytes 6062080 | tf_op jit(solution)/shard_map/dot_general | solution.py:80
  85.2 1.1 %fusion.2 = f32[40,8,8,128]{3,2,1,0:T(8,128)S(1)} fusion(f32[1024,320]{0,1:T(8,128)S(1)} %convolution_add_fusion.1, bf16[1024,1280]{1,0:T(8,128)(2,1)S(1)} %bitcast.70, bf16[9,1280,320]{1,2,0:T(8,128)(2,1)S(1)} %bitcast.81), kind=kOutput, calls=%fused_computation.13 | convolution fusion | flops 839188480 | bytes 6062080 | tf_op jit(solution)/shard_map/dot_general | solution.py:80
  86.2 0.2 fusion.5
  86.5 0.2 broadcast_in_dim.41
  86.7 1.9 %copy.52 = bf16[16,128,320]{2,0,1:T(8,128)(2,1)} copy(bf16[16,128,320]{1,2,0:T(8,128)(2,1)S(1)} %bitcast.69) | data formatting | bytes 2621440 | tf_op jit(solution)/shard_map/reshape | solution.py:84
  88.6 1.7 %broadcast_in_dim.42 = bf16[16,128,2,320]{3,0,2,1:T(8,128)(2,1)S(1)} broadcast(bf16[16,128,320]{2,0,1:T(8,128)(2,1)} %copy.52), dimensions={0,1,3} | broadcast | bytes 3932160 | tf_op jit(solution)/shard_map/broadcast_in_dim | solution.py:84
  90.3 3.1 %copy.53 = bf16[16,256,320]{1,2,0:T(8,128)(2,1)} copy(bf16[16,256,320]{2,0,1:T(8,128)(2,1)S(1)} %bitcast.68) | data formatting | bytes 5242880
  (7 shorter events, 0.1 us)
Async XLA Ops:
  7.2 11.4 %copy-start = (bf16[8,128,320]{1,2,0:T(8,128)(2,1)S(1)}, bf16[8,128,320]{1,2,0:T(8,128)(2,1)}, u32[]{:S(2)}) copy-start(bf16[8,128,320]{1,2,0:T(8,128)(2,1)} %param.11) | copy-start | bytes 1966084
  7.2 11.7 %copy-start.3 = (s32[1280]{0:T(1024)S(1)}, s32[1280]{0:T(1024)}, u32[]{:S(2)}) copy-start(s32[1280]{0:T(1024)} %param.15) | copy-start | bytes 15364
  7.2 39.0 %copy-start.6 = (f32[1,32]{1,0:T(1,128)S(1)}, f32[1,32]{1,0:T(1,128)}, u32[]{:S(2)}) copy-start(f32[1,32]{1,0:T(1,128)} %param.21) | copy-start | bytes 388
  7.2 39.0 %copy-start.8 = (f32[1,32]{1,0:T(1,128)S(1)}, f32[1,32]{1,0:T(1,128)}, u32[]{:S(2)}) copy-start(f32[1,32]{1,0:T(1,128)} %param.20) | copy-start | bytes 388
  7.2 39.0 %copy-start.7 = (f32[32]{0:T(128)S(1)}, f32[32]{0:T(128)}, u32[]{:S(2)}) copy-start(f32[32]{0:T(128)} %param.19) | copy-start | bytes 388
  7.2 39.0 %copy-start.9 = (f32[32]{0:T(128)S(1)}, f32[32]{0:T(128)}, u32[]{:S(2)}) copy-start(f32[32]{0:T(128)} %param.18) | copy-start | bytes 388
  7.2 39.7 %copy-start.4 = (f32[1280]{0:T(1024)S(1)}, f32[1280]{0:T(1024)}, u32[]{:S(2)}) copy-start(f32[1280]{0:T(1024)} %param.14) | copy-start | bytes 15364
  7.2 39.7 %copy-start.5 = (f32[1280]{0:T(1024)S(1)}, f32[1280]{0:T(1024)}, u32[]{:S(2)}) copy-start(f32[1280]{0:T(1024)} %param.13) | copy-start | bytes 15364
  7.2 50.8 %all-gather.2.cloned.1.call-start = ((), (), s32[]{:S(2)}) async-start(), calls=%async_computation | async-start | bytes 3276800 | tf_op jit(solution)/shard_map/all_gather | solution.py:69
  10.8 36.1 %collective-permute-start.1 = (bf16[1,128,320]{1,0,2:T(2,128)(2,1)S(1)}, bf16[1,128,320]{1,0,2:T(2,128)(2,1)S(1)}, u32[]{:S(2)}, u32[]{:S(2)}) collective-permute-start(bf16[1,128,320]{1,0,2:T(2,128)(2,1)S(1)} %copy.55), channel_id=1, source_target_pairs={{4,0},{8,4},{12,8},{16,12},{20,16},{24,20},{28,24},{5,1},{9,5},{13... | collective-permute-start | bytes 245768 | tf_op jit(solution)/shard_map/ppermute | solution.py:17
  12.2 34.7 %collective-permute-start = (bf16[1,128,320]{1,0,2:T(2,128)(2,1)S(1)}, bf16[1,128,320]{1,0,2:T(2,128)(2,1)S(1)}, u32[]{:S(2)}, u32[]{:S(2)}) collective-permute-start(bf16[1,128,320]{1,0,2:T(2,128)(2,1)S(1)} %copy.54), channel_id=1, source_target_pairs={{0,4},{4,8},{8,12},{12,16},{16,20},{20,24},{24,28},{1,5},{5,9},{9,... | collective-permute-start | bytes 245768 | tf_op jit(solution)/shard_map/ppermute | solution.py:14
  61.8 1.7 %copy-start.1 = (bf16[1,128,1280]{2,1,0:T(8,128)(2,1)S(1)}, bf16[1,128,1280]{2,1,0:T(8,128)(2,1)}, u32[]{:S(2)}) copy-start(bf16[1,128,1280]{2,1,0:T(8,128)(2,1)} %copy.56) | copy-start | bytes 983044
  61.9 1.7 %copy-start.2 = (bf16[1,128,1280]{2,1,0:T(8,128)(2,1)S(1)}, bf16[1,128,1280]{2,1,0:T(8,128)(2,1)}, u32[]{:S(2)}) copy-start(bf16[1,128,1280]{2,1,0:T(8,128)(2,1)} %copy.57) | copy-start | bytes 983044
  74.1 4.7 %slice-start = ((s8[7372800]{0:T(1024)(128)(4,1)}), s8[4194304]{0:T(1024)(128)(4,1)S(1)}, s32[]{:S(2)}) async-start(s8[7372800]{0:T(1024)(128)(4,1)} %bitcast.80), calls=%async_computation.1 | async-start | bytes 8388608
  76.4 2.4 %slice-start.1 = ((s8[7372800]{0:T(1024)(128)(4,1)}), s8[3178496]{0:T(1024)(128)(4,1)S(1)}, s32[]{:S(2)}) async-start(s8[7372800]{0:T(1024)(128)(4,1)} %bitcast.80), calls=%async_computation.2 | async-start | bytes 6356992
Sparse Core Ops, SparseCore 0:
  10.2 28.4 all-gather.1
where the time goes:
time: 101 us; the launch traced here: 100 us
  blocking collectives  34.6 us (34%)
  local copies, waits for them, and re-layouts  27.7 us (27%)
  between operations  15.1 us (15%)
  matrix products  12 us (12%)
  starting transfers between devices  6.87 us (7%)
  other arithmetic  3.98 us (4%)
    psum x1, blocking collectives, per_device(): image_one, image_two = lax.psum((strip_one, strip_two), 'strip')  19.8 us
    dot_general x9, matrix products, per_device(): jnp.dot(patch, weight[tap], preferred_element_type=jnp.float32)  12 us
    slice x1, local copies, waits for them, and re-layouts, per_device(): padded[down:down + rows, across:across + width].reshape(rows * width, depth)  10 us
    unnamed x30, local copies, waits for them, and re-layouts  8.07 us
    all_gather x1, blocking collectives, per_device(): bound = lax.all_gather(bounds, 'chan', axis=2, tiled=True)  7.51 us
    psum x1, blocking collectives, per_device(): strip_one, strip_two = lax.psum((part_one, part_two), 'chan')  7.31 us
    ppermute x1, starting transfers between devices, padded_2(): lax.ppermute(lax.slice_in_dim(block, block.shape[dim] - width, None, axis...  5.54 us
    all_gather x1, local copies, waits for them, and re-layouts, per_device(): piece = lax.all_gather(activations, 'chan', axis=2, tiled=True)  3.82 us
  transfers between devices with their start and end apart: 3, of which 0 were waited for; matrix products, arithmetic and copies ran while one was open for 6% of the time, Pallas kernels for 0%

commit v1 on v0

v1 whole, which is shorter than its diff:
```python
import functools

import jax
import jax.numpy as jnp
from jax import lax
from jax.experimental import pallas as pl
from jax.experimental.pallas import tpu as pltpu
from jax.sharding import PartitionSpec as P


EPS = 1e-05
EARLY = 4
HI = lax.Precision.HIGHEST
VMEM = pltpu.VMEM
MIB = 1 << 20


def spec(space=VMEM):
    return pl.BlockSpec(memory_space=space)


def to_column(row):
    n = row.shape[1]
    same = lax.broadcasted_iota(jnp.int32, (n, n), 0) == lax.broadcasted_iota(jnp.int32, (n, n), 1)
    return jnp.sum(jnp.where(same, row, 0.0), axis=1, keepdims=True)


def to_row(column):
    n = column.shape[0]
    same = lax.broadcasted_iota(jnp.int32, (n, n), 0) == lax.broadcasted_iota(jnp.int32, (n, n), 1)
    return jnp.sum(jnp.where(same, column, 0.0), axis=0, keepdims=True)


def lane(sums, at):
    lanes = lax.broadcasted_iota(jnp.int32, sums.shape, 1)
    return jnp.sum(jnp.where(lanes == at, sums, 0.0), axis=1, keepdims=True)


def split(sums):
    first = sums.astype(jnp.bfloat16)
    rest = sums - first.astype(jnp.float32)
    second = rest.astype(jnp.bfloat16)
    third = (rest - second.astype(jnp.float32)).astype(jnp.bfloat16)
    return first, second, third


def put_sums(ref, row, sums):
    n = sums.shape[0]
    for i, piece in enumerate(split(sums)):
        ref[row, i * n : (i + 1) * n, :] = piece


def get_sums(ref, row, n):
    pieces = [ref[row, i * n : (i + 1) * n, :].astype(jnp.float32) for i in range(3)]
    return pieces[0] + (pieces[1] + pieces[2])


def stats_kernel(
    n_chan, groups, where_ref, gm_ref, x_ref, edge_ref, head_ref, tail_ref, near_ref, part_ref, in_ref, s_ref, sems
):
    rows, local_c, width = x_ref.shape
    length, me, odd = where_ref[0], where_ref[1], where_ref[2]
    early = head_ref.shape[0] - 1
    copies = [
        pltpu.make_async_copy(x_ref, in_ref, sems.at[0]),
        pltpu.make_async_copy(edge_ref.at[1 - odd], near_ref.at[0], sems.at[1]),
    ]
    for copy in copies:
        copy.start()
    copies[0].wait()
    step = 64
    for at in range(0, local_c, step):
        one = jnp.zeros((step, width), jnp.float32)
        two = jnp.zeros((step, width), jnp.float32)
        for r in range(rows):
            value = in_ref[r, at : at + step, :]
            if r < early:
                head_ref[r, at : at + step, :] = value
            else:
                tail_ref[r - early, at : at + step, :] = value
            value = jnp.where(r < length, value.astype(jnp.float32), 0.0)
            one = one + value
            two = two + value * value
        s_ref[at : at + step, :width] = one
        s_ref[at : at + step, width:] = two
    mine = gm_ref[:, :local_c]
    for k in range(1, n_chan):
        mine = jnp.where(me == k, gm_ref[:, k * local_c : (k + 1) * local_c], mine)
    member = (lax.broadcasted_iota(jnp.int32, (groups, local_c), 0) == mine).astype(jnp.float32)
    sums = jnp.dot(member, s_ref[...], precision=HI, preferred_element_type=jnp.float32)
    one = jnp.sum(sums[:, :width], axis=1, keepdims=True)
    two = jnp.sum(sums[:, width:], axis=1, keepdims=True)
    lanes = lax.broadcasted_iota(jnp.int32, part_ref.shape, 1)
    part = jnp.where(lanes == 0, one, jnp.where(lanes == 1, two, 0.0))
    part_ref[...] = part
    put_sums(head_ref, early, part)
    put_sums(near_ref, 1, part)
    copies[1].wait()


def far_kernel(where_ref, near_ref, part_ref, edge_ref, far_ref, pair_ref, sem):
    copy = pltpu.make_async_copy(edge_ref.at[where_ref[2]], far_ref.at[0], sem)
    copy.start()
    pair = part_ref[...] + get_sums(near_ref, 1, part_ref.shape[0])
    pair_ref[...] = pair
    put_sums(far_ref, 1, pair)
    copy.wait()


def halo_kernel(where_ref, near_ref, far_ref, mine_ref, other_ref, out_ref):
    odd, strip, n_strip = where_ref[2], where_ref[3], where_ref[4]
    near, far = near_ref[0], far_ref[0]
    above = jnp.where(odd == 1, near, far)
    below = jnp.where(odd == 1, far, near)
    zero = jnp.zeros_like(near)
    out_ref[0] = jnp.where(strip == 0, zero, above)
    out_ref[1] = jnp.where(strip == n_strip - 1, zero, below)
    put_sums(out_ref, 2, mine_ref[...] + other_ref[...])


def conv_kernel(
    n_chan,
    per_group,
    total,
    where_ref,
    part_ref,
    smean_ref,
    ssquare_ref,
    omean_ref,
    osquare_ref,
    gm_ref,
    gamma_ref,
    beta_ref,
    *refs,
):
    x_any, w_any, refs = refs[0], refs[1], refs[2:]
    m_refs, refs = (None,) + refs[: n_chan - 1], refs[n_chan - 1 :]
    t_refs, refs = (None,) + refs[: n_chan - 1], refs[n_chan - 1 :]
    h_refs, refs = refs[:n_chan], refs[n_chan:]
    out_ref, mean_ref, square_ref, x_ref, w_ref, a_ref, ss_ref, o_ref, sem, sems = refs
    rows, local_c, width = x_ref.shape
    early = m_refs[1].shape[0] - 1
    copies = [pltpu.make_async_copy(x_any, x_ref, sems.at[0])]
    for dy in range(3):
        copies.append(pltpu.make_async_copy(w_any.at[dy], w_ref.at[dy], sems.at[1 + dy]))
    for copy in copies:
        copy.start()

    def source(k, r):
        if k == 0:
            return x_ref, r
        return (m_refs[k], r) if r < early else (t_refs[k], r - early)

    channels = n_chan * local_c
    groups = smean_ref.shape[1]
    length, me = where_ref[0], where_ref[1]
    image = get_sums(h_refs[0], 2, groups)
    strip = part_ref[...]
    for k in range(1, n_chan):
        image = image + get_sums(h_refs[k], 2, groups)
        strip = strip + get_sums(m_refs[k], early, groups)
    mean_ref[...] = to_row(lane(image, 0)) / total
    square_ref[...] = to_row(lane(image, 1)) / total

    count = length.astype(jnp.float32) * (width * per_group)
    count = jnp.full((groups, 1), count, jnp.float32)
    fresh_mean = lane(strip, 0) / count
    fresh_square = lane(strip, 1) / count
    mean = to_column(smean_ref[...]) + fresh_mean - to_column(omean_ref[...])
    square = to_column(ssquare_ref[...]) + fresh_square - to_column(osquare_ref[...])
    var = jnp.maximum(square - mean * mean, 0.5 * (fresh_square - fresh_mean * fresh_mean))
    rstd = lax.rsqrt(var + EPS)
    member = lax.broadcasted_iota(jnp.int32, (groups, channels), 0) == gm_ref[...]
    left = jnp.where(member, gamma_ref[...], 0.0)
    first = lax.broadcasted_iota(jnp.int32, (8, channels), 0) == 0
    left = jnp.concatenate([left, jnp.where(first, beta_ref[...], 0.0)], axis=0)
    ones = (lax.broadcasted_iota(jnp.int32, (8, width), 0) == 0).astype(jnp.float32)
    right = jnp.concatenate(
        [
            jnp.concatenate([jnp.broadcast_to(rstd, (groups, width)), jnp.broadcast_to(-mean * rstd, (groups, width))], axis=1),
            jnp.concatenate([jnp.zeros_like(ones), ones], axis=1),
        ],
        axis=0,
    )
    ss_ref[...] = lax.dot_general(
        left, right, (((0,), (0,)), ((), ())), precision=HI, preferred_element_type=jnp.float32
    )

    zero = jnp.zeros((channels, width), jnp.bfloat16)
    a_ref[rows + 1] = zero
    copies[0].wait()
    for k in range(n_chan):
        owner = jnp.bitwise_xor(me, k)
        base = pl.multiple_of(owner * local_c, 64)
        a_ref[0, pl.ds(base, local_c), :] = h_refs[k][0]
        step = 64
        for at in range(0, local_c, step):
            here = pl.ds(pl.multiple_of(base + at, 64), step)
            scale = ss_ref[here, :width]
            shift = ss_ref[here, width:]
            for r in range(rows):
                from_ref, place = source(k, r)
                value = from_ref[place, at : at + step, :].astype(jnp.float32) * scale + shift
                half = 0.5 * value
                act = half * jnp.tanh(half) + half
                act = jnp.where(r < length, act, 0.0).astype(jnp.bfloat16)
                a_ref[r + 1, here, :] = act
        a_ref[length + 1, pl.ds(base, local_c), :] = h_refs[k][1]

    lanes = lax.broadcasted_iota(jnp.int32, (local_c, width), 1)
    double = (
        lax.broadcasted_iota(jnp.int32, (width, 2 * width), 0)
        == lax.div(lax.broadcasted_iota(jnp.int32, (width, 2 * width), 1), 2)
    ).astype(jnp.bfloat16)
    per = 2
    for copy in copies[1:]:
        copy.wait()

    def block(b, carry):
        r0 = b * per
        acc = None
        for dy in range(3):
            right = jnp.concatenate([a_ref[r0 + dy + i] for i in range(per)], axis=1)
            part = jnp.dot(w_ref[dy], right, preferred_element_type=jnp.float32)
            acc = part if acc is None else acc + part
        for i in range(per):
            r = r0 + i
            cut = slice(i * width, (i + 1) * width)
            low = acc[:local_c, cut]
            mid = acc[local_c : 2 * local_c, cut]
            high = acc[2 * local_c :, cut]
            low = jnp.where(lanes == 0, 0.0, pltpu.roll(low, 1, 1))
            high = jnp.where(lanes == width - 1, 0.0, pltpu.roll(high, width - 1, 1))
            value = x_ref[r].astype(jnp.float32) + (mid + low + high)
            value = jnp.where(r < length, value, 0.0).astype(jnp.bfloat16)
            wide = jnp.dot(value, double, preferred_element_type=jnp.float32)
            o_ref[r] = wide.astype(jnp.bfloat16)
            for a in range(2):
                pltpu.make_async_copy(o_ref.at[r], out_ref.at[2 * r + a], sem).start()
        return carry

    lax.fori_loop(0, rows // per, block, 0)
    for r in range(rows):
        for a in range(2):
            pltpu.make_async_copy(o_ref.at[r], out_ref.at[2 * r + a], sem).wait()


def pairs(count, k):
    return [(i, i ^ k) for i in range(count)]


def per_device(
    activations,
    weight,
    gamma,
    beta,
    group_map,
    lengths,
    stale_edges,
    stale_mean,
    stale_square,
    old_mean,
    old_square,
):
    rows, width, local_c = activations.shape
    taps, channels, _ = weight.shape
    groups = stale_mean.shape[0]
    per_group = channels // groups
    n_chan, n_strip = lax.axis_size("chan"), lax.axis_size("strip")
    me, strip = lax.axis_index("chan"), lax.axis_index("strip")
    total = float(n_strip * (3 * rows // 4) * width * per_group)
    x = jnp.swapaxes(activations, 1, 2)
    w = jnp.swapaxes(weight, 1, 2).reshape(3, 3 * local_c, channels)
    edges = jnp.swapaxes(stale_edges, 1, 2)
    gm = group_map.reshape(1, channels)
    where = jnp.stack(
        [lengths[0], me.astype(jnp.int32), lax.rem(strip, 2).astype(jnp.int32), strip.astype(jnp.int32), jnp.int32(n_strip)]
    )
    early = EARLY
    bf16, f32 = jnp.bfloat16, jnp.float32
    row = (local_c, width)

    def shape(n):
        return jax.ShapeDtypeStruct((n, *row), bf16)

    def chan(value, k):
        return lax.ppermute(value, "chan", pairs(n_chan, k))

    sums = jax.ShapeDtypeStruct((groups, 128), f32)
    head, tail, near_out, part = pl.pallas_call(
        functools.partial(stats_kernel, n_chan, groups),
        out_shape=(shape(early + 1), shape(rows - early), shape(2), sums),
        in_specs=[spec(pltpu.SMEM), spec(), spec(pl.ANY), spec(pl.ANY)],
        out_specs=(spec(),) * 4,
        scratch_shapes=[
            VMEM((rows, *row), bf16),
            VMEM((local_c, 2 * width), f32),
            pltpu.SemaphoreType.DMA((2,)),
        ],
        compiler_params=pltpu.CompilerParams(vmem_limit_bytes=8 * MIB),
        name="stats",
    )(where, gm, x, edges)
    heads = {1: chan(head, 1), 2: chan(head, 2)}
    tails = {1: chan(tail, 1), 2: chan(tail, 2)}
    heads[3] = chan(heads[2], 1)
    tails[3] = chan(tails[2], 1)

    near = lax.ppermute(near_out, "strip", pairs(n_strip, 1))
    far_out, pair = pl.pallas_call(
        far_kernel,
        out_shape=(shape(2), sums),
        in_specs=[spec(pltpu.SMEM), spec(), spec(), spec(pl.ANY)],
        out_specs=(spec(),) * 2,
        scratch_shapes=[pltpu.SemaphoreType.DMA],
        compiler_params=pltpu.CompilerParams(vmem_limit_bytes=4 * MIB),
        name="farmsg",
    )(where, near, part, edges)
    ring = [(i, (((i + 1) ^ 1) - 1) % n_strip) for i in range(n_strip)]
    far = lax.ppermute(far_out, "strip", ring)
    mine = pair + sum(far[1, i * groups : (i + 1) * groups].astype(f32) for i in range(3))
    k = 4
    other = lax.ppermute(mine, "strip", pairs(n_strip, k))
    while 2 * k < n_strip:
        k *= 2
        mine = mine + other
        other = lax.ppermute(mine, "strip", pairs(n_strip, k))
    halo = pl.pallas_call(
        halo_kernel,
        out_shape=shape(3),
        in_specs=[spec(pltpu.SMEM)] + [spec()] * 4,
        out_specs=spec(),
        compiler_params=pltpu.CompilerParams(vmem_limit_bytes=4 * MIB),
        name="halo",
    )(where, near, far, mine, other)
    halos = [halo, chan(halo, 1), chan(halo, 2)]
    halos.append(chan(halos[2], 1))

    out, new_mean, new_square = pl.pallas_call(
        functools.partial(conv_kernel, n_chan, per_group, total),
        out_shape=(
            jax.ShapeDtypeStruct((2 * rows, local_c, 2 * width), bf16),
            jax.ShapeDtypeStruct((1, groups), f32),
            jax.ShapeDtypeStruct((1, groups), f32),
        ),
        in_specs=[spec(pltpu.SMEM)] + [spec()] * 8 + [spec(pl.ANY)] * 2 + [spec()] * (3 * n_chan - 2),
        out_specs=(spec(pl.ANY), spec(), spec()),
        scratch_shapes=[
            VMEM((rows, *row), bf16),
            VMEM((3, 3 * local_c, channels), bf16),
            VMEM((rows + 2, channels, width), bf16),
            VMEM((channels, 2 * width), f32),
            VMEM((rows, local_c, 2 * width), bf16),
            pltpu.SemaphoreType.DMA,
            pltpu.SemaphoreType.DMA((4,)),
        ],
        compiler_params=pltpu.CompilerParams(vmem_limit_bytes=32 * MIB),
        cost_estimate=pl.CostEstimate(
            flops=2 * rows * width * taps * channels * local_c,
            bytes_accessed=taps * channels * local_c * 2,
            transcendentals=rows * width * channels,
        ),
        name="conv",
    )(
        where,
        part,
        stale_mean.reshape(1, groups),
        stale_square.reshape(1, groups),
        old_mean,
        old_square,
        gm,
        gamma.reshape(1, channels),
        beta.reshape(1, channels),
        x,
        w,
        *[heads[k] for k in range(1, n_chan)],
        *[tails[k] for k in range(1, n_chan)],
        *halos,
    )
    upsampled = jnp.swapaxes(out, 1, 2)
    return (upsampled, new_mean.reshape(groups), new_square.reshape(groups))


def solution(mesh):
    in_specs = (
        P("strip", None, "chan"),
        P(None, None, "chan"),
        P(),
        P(),
        P(),
        P("strip"),
        P("strip", None, "chan"),
        P(),
        P(),
        P("strip", None),
        P("strip", None),
    )
    out_specs = (P("strip", None, "chan"), P(), P())
    return jax.shard_map(
        per_device, mesh=mesh, in_specs=in_specs, out_specs=out_specs, check_vma=False
    )
```

time: 101 us -> 65.5 us (0.65)
  blocking collectives: 34.6 us -> 0 us
  waiting for transfers between devices: 0.02 us -> 20.9 us
  Pallas kernels: 0 us -> 18.8 us
  local copies, waits for them, and re-layouts: 27.7 us -> 11 us
  between operations: 15.1 us -> 1.35 us
  matrix products: 12 us -> 0 us
  starting transfers between devices: 6.87 us -> 13.1 us
  other arithmetic: 3.98 us -> 0.01 us
    psum x2 -> x0, blocking collectives: 27.1 us -> none  [the longest x1 19.8 us: per_device(): image_one, image_two = lax.psum((strip_one, strip_two), 'strip')]
    ppermute x2 -> x12, waiting for transfers between devices: 0.01 us -> 20.9 us  [the longest x9 11.6 us: chan(): return lax.ppermute(value, 'chan', pairs(n_chan, k))]
    pallas_call x0 -> x4, Pallas kernels: none -> 18.8 us  [the longest x1 15.9 us: per_device(): pl.pallas_call(functools.partial(conv_kernel, n_chan, per_group, total),...]
    dot_general x9 -> x0, matrix products: 12 us -> none  [per_device(): jnp.dot(patch, weight[tap], preferred_element_type=jnp.float32)]
    slice x3 -> x0, local copies, waits for them, and re-layouts: 11.9 us -> none  [the longest x1 10 us: per_device(): padded[down:down + rows, across:across + width].reshape(rows * width, depth)]
    all_gather x1 -> x0, blocking collectives: 7.51 us -> none  [per_device(): bound = lax.all_gather(bounds, 'chan', axis=2, tiled=True)]
    ppermute x2 -> x12, starting transfers between devices: 6.83 us -> 13.1 us  [the longest x1 4.84 us: per_device(): far = lax.ppermute(far_out, 'strip', ring)]
    all_gather x1 -> x0, local copies, waits for them, and re-layouts: 3.82 us -> none  [per_device(): piece = lax.all_gather(activations, 'chan', axis=2, tiled=True)]
  transfers between devices with their start and end apart: 3 -> 12, of which waited for: 0 -> 7; matrix products, arithmetic and copies ran while one was open for 6% -> 2% of each run, Pallas kernels for 0% -> 1%
where the time goes in v1:
time: 65.5 us; the launch traced here: 65 us
  waiting for transfers between devices  20.9 us (32%)
  Pallas kernels  18.8 us (29%)
  starting transfers between devices  13.1 us (20%)
  local copies, waits for them, and re-layouts  11 us (17%)
  between operations  1.35 us (2%)
    pallas_call x1, Pallas kernels, per_device(): pl.pallas_call(functools.partial(conv_kernel, n_chan, per_group, total),...  15.9 us
    ppermute x9, waiting for transfers between devices, chan(): return lax.ppermute(value, 'chan', pairs(n_chan, k))  11.6 us
    unnamed x16, local copies, waits for them, and re-layouts  8.8 us
    ppermute x1, starting transfers between devices, per_device(): far = lax.ppermute(far_out, 'strip', ring)  4.84 us
    ppermute x9, starting transfers between devices, chan(): return lax.ppermute(value, 'chan', pairs(n_chan, k))  4.22 us
    ppermute x1, waiting for transfers between devices, per_device(): near = lax.ppermute(near_out, 'strip', pairs(n_strip, 1))  4.2 us
    ppermute x1, waiting for transfers between devices, per_device(): other = lax.ppermute(mine, 'strip', pairs(n_strip, k))  3.73 us
    ppermute x1, starting transfers between devices, per_device(): near = lax.ppermute(near_out, 'strip', pairs(n_strip, 1))  3.06 us
  transfers between devices with their start and end apart: 12, of which 7 were waited for; matrix products, arithmetic and copies ran while one was open for 2% of the time, Pallas kernels for 1%

profile of v1, /device:TPU:0, one launch (start us, length us, event | category | flops | bytes accessed | tf_op | source)
XLA Modules:
  0.0 65.0 jit_solution(16742963430055465234)
XLA Ops:
  1.3 0.7 %reshape.35.gm_ref = s32[1,1280]{1,0:T(1,128)S(1)} reshape(s32[1280]{0:T(1024)} %param.15) | data formatting | bytes 10240 | tf_op jit(solution)/shard_map/reshape | solution.py:275
  2.0 0.1 stack.15.where_ref
  2.1 0.0 copy-start
  2.1 1.1 %copy-done = bf16[8,128,320]{1,2,0:T(8,128)(2,1)S(1)} copy-done((bf16[8,128,320]{1,2,0:T(8,128)(2,1)S(1)}, bf16[8,128,320]{1,2,0:T(8,128)(2,1)}, u32[]{:S(2)}) %copy-start) | copy-done | bytes 655384
  3.2 0.0 copy-start.2
  3.2 0.9 %copy-done.2 = bf16[2,128,320]{1,2,0:T(8,128)(2,1)S(1)} copy-done((bf16[2,128,320]{1,2,0:T(8,128)(2,1)S(1)}, bf16[2,128,320]{1,2,0:T(8,128)(2,1)}, u32[]{:S(2)}) %copy-start.2) | copy-done | bytes 163864
  4.1 1.6 %stats.1 = (bf16[5,320,128]{2,1,0:T(8,128)(2,1)S(1)}, bf16[4,320,128]{2,1,0:T(8,128)(2,1)S(1)}, bf16[2,320,128]{2,1,0:T(8,128)(2,1)S(1)}, f32[32,128]{1,0:T(8,128)S(1)}) custom-call(s32[5]{0:T(128)S(1)} %stack.15.where_ref, s32[1,1280]{1,0:T(1,128)S(1)} %reshape.35.gm_ref, bf16[8,320,128]{2,1,0:T(8,128)(2,1)S(1)} %bitcast.15, bf16[2,320,128]{2,1,0:T(8,128)(2,1)S(1)} %bitcast.17), custom_call_target="tpu_custom_call" | custom-call | tf_op jit(solution)/shard_map/stats/pallas_call | solution.py:290
  5.7 3.1 %collective-permute-start.6 = (bf16[2,320,128]{2,1,0:T(8,128)(2,1)S(1)}, bf16[2,320,128]{2,1,0:T(8,128)(2,1)S(1)}, u32[]{:S(2)}, u32[]{:S(2)}) collective-permute-start(bf16[2,320,128]{2,1,0:T(8,128)(2,1)S(1)} %get-tuple-element.15), channel_id=1, source_target_pairs={{0,4},{4,0},{8,12},{12,8},{16,20},{20,16},{24,28},{28,24},{1,5},{5... | collective-permute-start | bytes 491528 | tf_op jit(solution)/shard_map/ppermute | solution.py:308
  8.8 4.2 %collective-permute-done.6.near_ref = bf16[2,320,128]{2,1,0:T(8,128)(2,1)S(1)} collective-permute-done((bf16[2,320,128]{2,1,0:T(8,128)(2,1)S(1)}, bf16[2,320,128]{2,1,0:T(8,128)(2,1)S(1)}, u32[]{:S(2)}, u32[]{:S(2)}) %collective-permute-start.6) | collective-permute-done | bytes 163872 | tf_op jit(solution)/shard_map/ppermute | solution.py:308
  13.0 0.7 %farmsg.1 = (bf16[2,320,128]{2,1,0:T(8,128)(2,1)S(1)}, f32[32,128]{1,0:T(8,128)S(1)}) custom-call(s32[5]{0:T(128)S(1)} %stack.15.where_ref, bf16[2,320,128]{2,1,0:T(8,128)(2,1)S(1)} %collective-permute-done.6.near_ref, f32[32,128]{1,0:T(8,128)S(1)} %get-tuple-element.12.part_ref, bf16[2,320,128]{2,1,0:T(8,128)(2,1)S(1)} %bitcast.18), custom_call_target="tpu_custom_call" | custom-call | tf_op jit(solution)/shard_map/farmsg/pallas_call | solution.py:309
  13.6 4.8 %collective-permute-start.7 = (bf16[2,320,128]{2,1,0:T(8,128)(2,1)S(1)}, bf16[2,320,128]{2,1,0:T(8,128)(2,1)S(1)}, u32[]{:S(2)}, u32[]{:S(2)}) collective-permute-start(bf16[2,320,128]{2,1,0:T(8,128)(2,1)S(1)} %get-tuple-element.16), channel_id=1, source_target_pairs={{0,28},{4,8},{8,4},{12,16},{16,12},{20,24},{24,20},{28,0},{1,29},{... | collective-permute-start | bytes 491528 | tf_op jit(solution)/shard_map/ppermute | solution.py:319
  18.5 1.5 %collective-permute-start.1 = (bf16[5,320,128]{2,1,0:T(8,128)(2,1)S(1)}, bf16[5,320,128]{2,1,0:T(8,128)(2,1)S(1)}, u32[]{:S(2)}, u32[]{:S(2)}) collective-permute-start(bf16[5,320,128]{2,1,0:T(8,128)(2,1)S(1)} %get-tuple-element.13), channel_id=1, source_target_pairs={{0,2},{1,3},{2,0},{3,1},{4,6},{5,7},{6,4},{7,5},{8,10},{9,11},{10,... | collective-permute-start | bytes 1228808 | tf_op jit(solution)/shard_map/ppermute | solution.py:287
  20.0 0.5 collective-permute-start.4
  20.5 0.0 collective-permute-start.3
  20.5 1.3 %collective-permute-done.7.far_ref = bf16[2,320,128]{2,1,0:T(8,128)(2,1)S(1)} collective-permute-done((bf16[2,320,128]{2,1,0:T(8,128)(2,1)S(1)}, bf16[2,320,128]{2,1,0:T(8,128)(2,1)S(1)}, u32[]{:S(2)}, u32[]{:S(2)}) %collective-permute-start.7) | collective-permute-done | bytes 163872 | tf_op jit(solution)/shard_map/ppermute | solution.py:319
  21.8 1.0 %collective-permute-start.8 = (f32[32,128]{1,0:T(8,128)S(1)}, f32[32,128]{1,0:T(8,128)S(1)}, u32[]{:S(2)}, u32[]{:S(2)}) collective-permute-start(f32[32,128]{1,0:T(8,128)S(1)} %bitcast_add_fusion.mine_ref), channel_id=1, source_target_pairs={{0,16},{4,20},{8,24},{12,28},{16,0},{20,4},{24,8},{28,12},{1,17},{... | collective-permute-start | bytes 49160 | tf_op jit(solution)/shard_map/ppermute | solution.py:322
  22.8 3.7 %collective-permute-done.8.other_ref = f32[32,128]{1,0:T(8,128)S(1)} collective-permute-done((f32[32,128]{1,0:T(8,128)S(1)}, f32[32,128]{1,0:T(8,128)S(1)}, u32[]{:S(2)}, u32[]{:S(2)}) %collective-permute-start.8) | collective-permute-done | bytes 16416 | tf_op jit(solution)/shard_map/ppermute | solution.py:322
  26.5 0.6 halo.1.refs_8_
  27.1 1.7 %collective-permute-start.10 = (bf16[3,320,128]{2,1,0:T(8,128)(2,1)S(1)}, bf16[3,320,128]{2,1,0:T(8,128)(2,1)S(1)}, u32[]{:S(2)}, u32[]{:S(2)}) collective-permute-start(bf16[3,320,128]{2,1,0:T(8,128)(2,1)S(1)} %halo.1.refs_8_), channel_id=1, source_target_pairs={{0,2},{1,3},{2,0},{3,1},{4,6},{5,7},{6,4},{7,5},{8,10},{9,11},{10,... | collective-permute-start | bytes 737288 | tf_op jit(solution)/shard_map/ppermute | solution.py:287
  28.8 0.0 collective-permute-start
  28.8 2.0 %collective-permute-done.1.refs_3_ = bf16[5,320,128]{2,1,0:T(8,128)(2,1)S(1)} collective-permute-done((bf16[5,320,128]{2,1,0:T(8,128)(2,1)S(1)}, bf16[5,320,128]{2,1,0:T(8,128)(2,1)S(1)}, u32[]{:S(2)}, u32[]{:S(2)}) %collective-permute-start.1) | collective-permute-done | bytes 409632 | tf_op jit(solution)/shard_map/ppermute | solution.py:287
  30.8 0.0 collective-permute-start.2
  30.8 7.0 %collective-permute-done.4.refs_6_ = bf16[4,320,128]{2,1,0:T(8,128)(2,1)S(1)} collective-permute-done((bf16[4,320,128]{2,1,0:T(8,128)(2,1)S(1)}, bf16[4,320,128]{2,1,0:T(8,128)(2,1)S(1)}, u32[]{:S(2)}, u32[]{:S(2)}) %collective-permute-start.4) | collective-permute-done | bytes 327712 | tf_op jit(solution)/shard_map/ppermute | solution.py:287
  37.8 0.0 collective-permute-start.5
  37.8 0.0 collective-permute-done.3.refs_5_
  37.9 0.5 collective-permute-start.9
  38.4 2.5 %collective-permute-done.10.refs_10_ = bf16[3,320,128]{2,1,0:T(8,128)(2,1)S(1)} collective-permute-done((bf16[3,320,128]{2,1,0:T(8,128)(2,1)S(1)}, bf16[3,320,128]{2,1,0:T(8,128)(2,1)S(1)}, u32[]{:S(2)}, u32[]{:S(2)}) %collective-permute-start.10) | collective-permute-done | bytes 245792 | tf_op jit(solution)/shard_map/ppermute | solution.py:287
  40.8 0.0 collective-permute-start.11
  40.8 0.7 %reshape.38.gamma_ref = f32[1,1280]{1,0:T(1,128)S(1)} reshape(f32[1280]{0:T(1024)} %param.13) | data formatting | bytes 10240 | tf_op jit(solution)/shard_map/reshape | solution.py:371
  41.5 0.7 %reshape.39.beta_ref = f32[1,1280]{1,0:T(1,128)S(1)} reshape(f32[1280]{0:T(1024)} %param.14) | data formatting | bytes 10240 | tf_op jit(solution)/shard_map/reshape | solution.py:372
  42.3 0.0 collective-permute-done.refs_2_
  42.3 0.0 collective-permute-done.9.refs_9_
  42.3 0.0 collective-permute-done.5.refs_7_
  42.3 0.0 collective-permute-done.2.refs_4_
  42.3 0.1 collective-permute-done.11.refs_11_
  42.4 0.0 copy-start.1
  42.4 1.1 %copy-done.1 = bf16[8,128,320]{1,2,0:T(8,128)(2,1)S(1)} copy-done((bf16[8,128,320]{1,2,0:T(8,128)(2,1)S(1)}, bf16[8,128,320]{1,2,0:T(8,128)(2,1)}, u32[]{:S(2)}) %copy-start.1) | copy-done | bytes 655384
  43.4 0.0 copy-start.3
  43.4 3.1 %copy-done.3 = bf16[9,1280,320]{1,2,0:T(8,128)(2,1)S(1)} copy-done((bf16[9,1280,320]{1,2,0:T(8,128)(2,1)S(1)}, bf16[9,1280,320]{1,2,0:T(8,128)(2,1)}, u32[]{:S(2)}) %copy-start.3) | copy-done | bytes 7372824
  46.5 0.0 copy-start.4
  46.5 0.7 %copy-done.4 = f32[32]{0:T(128)S(1)} copy-done((f32[32]{0:T(128)S(1)}, f32[32]{0:T(128)}, u32[]{:S(2)}) %copy-start.4) | copy-done | bytes 152
  47.2 0.0 copy-start.5
  47.2 0.7 %copy-done.5 = f32[32]{0:T(128)S(1)} copy-done((f32[32]{0:T(128)S(1)}, f32[32]{0:T(128)}, u32[]{:S(2)}) %copy-start.5) | copy-done | bytes 152
  47.9 0.0 copy-start.6
  47.9 0.7 %copy-done.6 = f32[1,32]{1,0:T(1,128)S(1)} copy-done((f32[1,32]{1,0:T(1,128)S(1)}, f32[1,32]{1,0:T(1,128)}, u32[]{:S(2)}) %copy-start.6) | copy-done | bytes 152
  48.5 0.0 copy-start.7
  48.5 0.7 %copy-done.7 = f32[1,32]{1,0:T(1,128)S(1)} copy-done((f32[1,32]{1,0:T(1,128)S(1)}, f32[1,32]{1,0:T(1,128)}, u32[]{:S(2)}) %copy-start.7) | copy-done | bytes 152
  49.2 15.9 %conv.1 = (bf16[16,320,256]{2,1,0:T(8,128)(2,1)}, f32[1,32]{1,0:T(1,128)}, f32[1,32]{1,0:T(1,128)}) custom-call(s32[5]{0:T(128)S(1)} %stack.15.where_ref, f32[32,128]{1,0:T(8,128)S(1)} %get-tuple-element.12.part_ref, f32[1,32]{1,0:T(1,128)S(1)} %bitcast.20, f32[1,32]{1,0:T(1,128)S(1)} %bitcast.21, f32[1,32]{1,0:T(1,128)S(1)} %copy-done.6, ...), custom_call_target="tpu_custom_call" | custom-call | flops 7549747200 | bytes 7372800 | tf_op jit(solution)/shard_map/conv/pallas_call | solution.py:338
  (1 shorter events, 0.0 us)
Async XLA Ops:
  2.1 1.1 %copy-start = (bf16[8,128,320]{1,2,0:T(8,128)(2,1)S(1)}, bf16[8,128,320]{1,2,0:T(8,128)(2,1)}, u32[]{:S(2)}) copy-start(bf16[8,128,320]{1,2,0:T(8,128)(2,1)} %param.11) | copy-start | bytes 1966084
  3.2 0.9 %copy-start.2 = (bf16[2,128,320]{1,2,0:T(8,128)(2,1)S(1)}, bf16[2,128,320]{1,2,0:T(8,128)(2,1)}, u32[]{:S(2)}) copy-start(bf16[2,128,320]{1,2,0:T(8,128)(2,1)} %param.17) | copy-start | bytes 491524
  5.7 7.3 %collective-permute-start.6 = (bf16[2,320,128]{2,1,0:T(8,128)(2,1)S(1)}, bf16[2,320,128]{2,1,0:T(8,128)(2,1)S(1)}, u32[]{:S(2)}, u32[]{:S(2)}) collective-permute-start(bf16[2,320,128]{2,1,0:T(8,128)(2,1)S(1)} %get-tuple-element.15), channel_id=1, source_target_pairs={{0,4},{4,0},{8,12},{12,8},{16,20},{20,16},{24,28},{28,24},{1,5},{5... | collective-permute-start | bytes 491528 | tf_op jit(solution)/shard_map/ppermute | solution.py:308
  13.6 8.2 %collective-permute-start.7 = (bf16[2,320,128]{2,1,0:T(8,128)(2,1)S(1)}, bf16[2,320,128]{2,1,0:T(8,128)(2,1)S(1)}, u32[]{:S(2)}, u32[]{:S(2)}) collective-permute-start(bf16[2,320,128]{2,1,0:T(8,128)(2,1)S(1)} %get-tuple-element.16), channel_id=1, source_target_pairs={{0,28},{4,8},{8,4},{12,16},{16,12},{20,24},{24,20},{28,0},{1,29},{... | collective-permute-start | bytes 491528 | tf_op jit(solution)/shard_map/ppermute | solution.py:319
  18.5 12.3 %collective-permute-start.1 = (bf16[5,320,128]{2,1,0:T(8,128)(2,1)S(1)}, bf16[5,320,128]{2,1,0:T(8,128)(2,1)S(1)}, u32[]{:S(2)}, u32[]{:S(2)}) collective-permute-start(bf16[5,320,128]{2,1,0:T(8,128)(2,1)S(1)} %get-tuple-element.13), channel_id=1, source_target_pairs={{0,2},{1,3},{2,0},{3,1},{4,6},{5,7},{6,4},{7,5},{8,10},{9,11},{10,... | collective-permute-start | bytes 1228808 | tf_op jit(solution)/shard_map/ppermute | solution.py:287
  20.0 17.9 %collective-permute-start.4 = (bf16[4,320,128]{2,1,0:T(8,128)(2,1)S(1)}, bf16[4,320,128]{2,1,0:T(8,128)(2,1)S(1)}, u32[]{:S(2)}, u32[]{:S(2)}) collective-permute-start(bf16[4,320,128]{2,1,0:T(8,128)(2,1)S(1)} %get-tuple-element.14), channel_id=1, source_target_pairs={{0,2},{1,3},{2,0},{3,1},{4,6},{5,7},{6,4},{7,5},{8,10},{9,11},{10,... | collective-permute-start | bytes 983048 | tf_op jit(solution)/shard_map/ppermute | solution.py:287
  20.5 17.3 %collective-permute-start.3 = (bf16[4,320,128]{2,1,0:T(8,128)(2,1)S(1)}, bf16[4,320,128]{2,1,0:T(8,128)(2,1)S(1)}, u32[]{:S(2)}, u32[]{:S(2)}) collective-permute-start(bf16[4,320,128]{2,1,0:T(8,128)(2,1)S(1)} %get-tuple-element.14), channel_id=1, source_target_pairs={{0,1},{1,0},{2,3},{3,2},{4,5},{5,4},{6,7},{7,6},{8,9},{9,8},{10,11... | collective-permute-start | bytes 983048 | tf_op jit(solution)/shard_map/ppermute | solution.py:287
  21.8 4.7 %collective-permute-start.8 = (f32[32,128]{1,0:T(8,128)S(1)}, f32[32,128]{1,0:T(8,128)S(1)}, u32[]{:S(2)}, u32[]{:S(2)}) collective-permute-start(f32[32,128]{1,0:T(8,128)S(1)} %bitcast_add_fusion.mine_ref), channel_id=1, source_target_pairs={{0,16},{4,20},{8,24},{12,28},{16,0},{20,4},{24,8},{28,12},{1,17},{... | collective-permute-start | bytes 49160 | tf_op jit(solution)/shard_map/ppermute | solution.py:322
  27.1 13.7 %collective-permute-start.10 = (bf16[3,320,128]{2,1,0:T(8,128)(2,1)S(1)}, bf16[3,320,128]{2,1,0:T(8,128)(2,1)S(1)}, u32[]{:S(2)}, u32[]{:S(2)}) collective-permute-start(bf16[3,320,128]{2,1,0:T(8,128)(2,1)S(1)} %halo.1.refs_8_), channel_id=1, source_target_pairs={{0,2},{1,3},{2,0},{3,1},{4,6},{5,7},{6,4},{7,5},{8,10},{9,11},{10,... | collective-permute-start | bytes 737288 | tf_op jit(solution)/shard_map/ppermute | solution.py:287
  28.8 13.5 %collective-permute-start = (bf16[5,320,128]{2,1,0:T(8,128)(2,1)S(1)}, bf16[5,320,128]{2,1,0:T(8,128)(2,1)S(1)}, u32[]{:S(2)}, u32[]{:S(2)}) collective-permute-start(bf16[5,320,128]{2,1,0:T(8,128)(2,1)S(1)} %get-tuple-element.13), channel_id=1, source_target_pairs={{0,1},{1,0},{2,3},{3,2},{4,5},{5,4},{6,7},{7,6},{8,9},{9,8},{10,11... | collective-permute-start | bytes 1228808 | tf_op jit(solution)/shard_map/ppermute | solution.py:287
  30.8 11.5 %collective-permute-start.2 = (bf16[5,320,128]{2,1,0:T(8,128)(2,1)S(1)}, bf16[5,320,128]{2,1,0:T(8,128)(2,1)S(1)}, u32[]{:S(2)}, u32[]{:S(2)}) collective-permute-start(bf16[5,320,128]{2,1,0:T(8,128)(2,1)S(1)} %collective-permute-done.1.refs_3_), channel_id=1, source_target_pairs={{0,1},{1,0},{2,3},{3,2},{4,5},{5,4},{6,7},{7,6},{8,9},{9,8},{10,11... | collective-permute-start | bytes 1228808 | tf_op jit(solution)/shard_map/ppermute | solution.py:287
  37.8 4.4 %collective-permute-start.5 = (bf16[4,320,128]{2,1,0:T(8,128)(2,1)S(1)}, bf16[4,320,128]{2,1,0:T(8,128)(2,1)S(1)}, u32[]{:S(2)}, u32[]{:S(2)}) collective-permute-start(bf16[4,320,128]{2,1,0:T(8,128)(2,1)S(1)} %collective-permute-done.4.refs_6_), channel_id=1, source_target_pairs={{0,1},{1,0},{2,3},{3,2},{4,5},{5,4},{6,7},{7,6},{8,9},{9,8},{10,11... | collective-permute-start | bytes 983048 | tf_op jit(solution)/shard_map/ppermute | solution.py:287
  37.9 4.4 %collective-permute-start.9 = (bf16[3,320,128]{2,1,0:T(8,128)(2,1)S(1)}, bf16[3,320,128]{2,1,0:T(8,128)(2,1)S(1)}, u32[]{:S(2)}, u32[]{:S(2)}) collective-permute-start(bf16[3,320,128]{2,1,0:T(8,128)(2,1)S(1)} %halo.1.refs_8_), channel_id=1, source_target_pairs={{0,1},{1,0},{2,3},{3,2},{4,5},{5,4},{6,7},{7,6},{8,9},{9,8},{10,11... | collective-permute-start | bytes 737288 | tf_op jit(solution)/shard_map/ppermute | solution.py:287
  40.8 1.5 %collective-permute-start.11 = (bf16[3,320,128]{2,1,0:T(8,128)(2,1)S(1)}, bf16[3,320,128]{2,1,0:T(8,128)(2,1)S(1)}, u32[]{:S(2)}, u32[]{:S(2)}) collective-permute-start(bf16[3,320,128]{2,1,0:T(8,128)(2,1)S(1)} %collective-permute-done.10.refs_10_), channel_id=1, source_target_pairs={{0,1},{1,0},{2,3},{3,2},{4,5},{5,4},{6,7},{7,6},{8,9},{9,8},{10,11... | collective-permute-start | bytes 737288 | tf_op jit(solution)/shard_map/ppermute | solution.py:287
  42.4 1.1 %copy-start.1 = (bf16[8,128,320]{1,2,0:T(8,128)(2,1)S(1)}, bf16[8,128,320]{1,2,0:T(8,128)(2,1)}, u32[]{:S(2)}) copy-start(bf16[8,128,320]{1,2,0:T(8,128)(2,1)} %param.11) | copy-start | bytes 1966084
  43.4 3.1 %copy-start.3 = (bf16[9,1280,320]{1,2,0:T(8,128)(2,1)S(1)}, bf16[9,1280,320]{1,2,0:T(8,128)(2,1)}, u32[]{:S(2)}) copy-start(bf16[9,1280,320]{1,2,0:T(8,128)(2,1)} %param.12) | copy-start | bytes 22118404
  46.5 0.7 %copy-start.4 = (f32[32]{0:T(128)S(1)}, f32[32]{0:T(128)}, u32[]{:S(2)}) copy-start(f32[32]{0:T(128)} %param.18) | copy-start | bytes 388
  47.2 0.7 %copy-start.5 = (f32[32]{0:T(128)S(1)}, f32[32]{0:T(128)}, u32[]{:S(2)}) copy-start(f32[32]{0:T(128)} %param.19) | copy-start | bytes 388
  47.9 0.7 %copy-start.6 = (f32[1,32]{1,0:T(1,128)S(1)}, f32[1,32]{1,0:T(1,128)}, u32[]{:S(2)}) copy-start(f32[1,32]{1,0:T(1,128)} %omean_ref.1) | copy-start | bytes 388
  48.5 0.7 %copy-start.7 = (f32[1,32]{1,0:T(1,128)S(1)}, f32[1,32]{1,0:T(1,128)}, u32[]{:S(2)}) copy-start(f32[1,32]{1,0:T(1,128)} %osquare_ref.1) | copy-start | bytes 388
